TPU v7x, 32 devices: a whole 2x2x4 slice. The times are simulated.
32 devices in a mesh: rep: 4 (over z), row: 4 (over x, core), col: 2 (over y).
Axes of the slice: x: 2, y: 2, z: 4, core: 2. Of those that a mesh axis runs over, the one named last changes fastest.
Arguments:
- grad_parts: bfloat16 [4, 16384, 6144], P('rep', ('row', 'col')), may hold values from -0.03125 to 0.03125, as said below
- statistic: float32 [6144, 6144], P('row', 'col'), may hold values from -150 to 150, as said below
Outputs:
- gram_matrix: float32 [6144, 6144], P('row', 'col')
- statistic_next: float32 [6144, 6144], P('row', 'col')
Inputs may be any that keep to these rules, and one draw needn't show every extreme that they name: Every entry of grad_parts has a magnitude between 2^-10 and 2^-5. statistic is symmetric and positive definite.
All inputs are finite; a program needn't handle non-finite values.
Results may differ from a plain program's by a relative error of at most 0.008.
Values may be sent and summed in bfloat16 or wider, within the bound.
A program may use at most 192 MiB of HBM per device.

v0:
```python
import jax
import jax.numpy as jnp
from jax import lax
from jax.sharding import PartitionSpec as P


def shards(grad_parts, statistic):
    own_part = grad_parts[0].astype(jnp.float32)
    summed = lax.psum_scatter(own_part.astype(jnp.bfloat16), "rep", scatter_dimension=0, tiled=True)
    rows_panel = lax.all_to_all(summed, "row", split_axis=1, concat_axis=0, tiled=True)
    cols_panel = lax.all_to_all(summed, "col", split_axis=1, concat_axis=0, tiled=True)
    row_count = lax.axis_size("row")
    col_count = lax.axis_size("col")
    quarter = summed.shape[0]
    left_whole = lax.all_gather(rows_panel, "col", axis=0, tiled=True)
    left_order = (
        left_whole.reshape(col_count, row_count, quarter, -1)
        .transpose(1, 0, 2, 3)
        .reshape(row_count * col_count * quarter, -1)
    )
    partial_tile = lax.dot_general(
        left_order,
        lax.all_gather(cols_panel, "row", axis=0, tiled=True),
        (((0,), (0,)), ((), ())),
        preferred_element_type=jnp.float32,
    )
    gram_tile = lax.psum(partial_tile, "rep")
    return (gram_tile, 0.95 * statistic + 0.05 * gram_tile)


def solution(mesh):
    return jax.shard_map(
        shards,
        mesh=mesh,
        in_specs=(P("rep", ("row", "col"), None), P("row", "col")),
        out_specs=(P("row", "col"), P("row", "col")),
        check_vma=False,
    )
```

profile of v0, /device:TPU:0, one launch (start us, length us, event | category | flops | bytes accessed | tf_op | source)
XLA Modules:
  0.0 1626.5 jit_solution(12246390620208611394)
XLA Ops:
  7.2 0.0 reduce-scatter.2.cloned.1.call-start
  7.2 30.3 %copy.5 = bf16[1,2048,6144]{1,2,0:T(8,128)(2,1)} copy(bf16[1,2048,6144]{2,1,0:T(8,128)(2,1)} %param.2) | data formatting | bytes 50331648 | tf_op args[0]
  37.5 0.0 reduce-scatter.2.cloned.1.call-update
  37.6 0.0 all-gather.3.cloned.1.call-start
  37.6 417.0 %reduce-scatter.2.cloned.1.call-done = bf16[512,6144]{0,1:T(8,128)(2,1)} async-done(((bf16[2048,6144]{0,1:T(8,128)(2,1)}), bf16[512,6144]{0,1:T(8,128)(2,1)}) %reduce-scatter.2.cloned.1.call-update) | async-done | bytes 6291472 | tf_op jit(solution)/shard_map/reduce_scatter | solution.py:9
  454.7 77.3 %all_to_all.38 = bf16[512,4,1536]{0,2,1:T(8,128)(2,1)} all-to-all(bf16[512,4,1536]{0,2,1:T(8,128)(2,1)} %bitcast.15), channel_id=1, replica_groups=mesh['rep'=4,'row'=4,'col'=2] {'row'}, dimensions={1} | all-to-all | bytes 12582912 | tf_op jit(solution)/shard_map/all_to_all | solution.py:10
  532.0 8.6 copy.6
  540.6 0.0 all-gather.3.cloned.1.call-update
  540.6 0.0 all-gather.5.cloned.1.call-start
  540.7 140.8 %all_to_all.39 = bf16[512,2,3072]{0,2,1:T(8,128)(2,1)} all-to-all(bf16[512,2,3072]{0,2,1:T(8,128)(2,1)} %bitcast.16), channel_id=1, replica_groups=mesh['rep'=4,'row'=4,'col'=2] {'col'}, dimensions={1} | all-to-all | bytes 12582912 | tf_op jit(solution)/shard_map/all_to_all | solution.py:11
  681.4 8.6 copy.8
  690.1 0.0 all-gather.5.cloned.1.call-update
  690.1 0.0 all-reduce.2.cloned.1.call-start
  690.2 64.5 %all-gather.3.cloned.1.call-done = bf16[4096,1536]{1,0:T(8,128)(2,1)} async-done(((bf16[2048,1536]{1,0:T(8,128)(2,1)}), bf16[4096,1536]{1,0:T(8,128)(2,1)}) %all-gather.3.cloned.1.call-update) | async-done | bytes 12582928 | tf_op jit(solution)/shard_map/all_gather | solution.py:15
  754.7 11.1 copy.7
  765.8 145.7 %all-gather.5.cloned.1.call-done = bf16[4096,3072]{1,0:T(8,128)(2,1)} async-done(((bf16[1024,3072]{1,0:T(8,128)(2,1)}), bf16[4096,3072]{1,0:T(8,128)(2,1)}) %all-gather.5.cloned.1.call-update) | async-done | bytes 25165840 | tf_op jit(solution)/shard_map/all_gather | solution.py:23
  911.5 48.0 %fusion = f32[1536,3072]{1,0:T(8,128)} fusion(bf16[4096,1536]{1,0:T(8,128)(2,1)} %bitcast.21, bf16[4096,3072]{1,0:T(8,128)(2,1)} %all-gather.5.cloned.1.call-done), kind=kOutput, calls=%fused_computation.1 | convolution fusion | flops 38654705664 | bytes 56623104 | tf_op jit(solution)/shard_map/dot_general | solution.py:21
  959.5 0.0 all-reduce.2.cloned.1.call-update
  959.6 629.5 %all-reduce.2.cloned.1.call-done = f32[1536,3072]{1,0:T(8,128)} async-done(((f32[1536,3072]{1,0:T(8,128)}), f32[1536,3072]{1,0:T(8,128)}) %all-reduce.2.cloned.1.call-update) | async-done | bytes 18874384 | tf_op jit(solution)/shard_map/psum | solution.py:27
  1589.1 0.0 copy-start
  1589.1 20.7 %multiply_add_fusion = f32[1536,3072]{1,0:T(8,128)} fusion(f32[1536,3072]{1,0:T(8,128)} %all-reduce.2.cloned.1.call-done, f32[1536,3072]{1,0:T(8,128)} %param.3), kind=kLoop, calls=%fused_computation | loop fusion | flops 14155776 | bytes 56623104 | tf_op jit(solution)/shard_map/add | solution.py:28
  1609.8 3.3 copy-done
  1613.1 6.8 copy.10
Async XLA Ops:
  7.2 447.5 %reduce-scatter.2.cloned.1.call-start = ((), (), s32[]{:S(2)}) async-start(), calls=%async_computation.3 | async-start | bytes 31457280 | tf_op jit(solution)/shard_map/reduce_scatter | solution.py:9
  37.6 717.1 %all-gather.3.cloned.1.call-start = ((), (), s32[]{:S(2)}) async-start(), calls=%async_computation.4 | async-start | bytes 18874368 | tf_op jit(solution)/shard_map/all_gather | solution.py:15
  540.6 370.9 %all-gather.5.cloned.1.call-start = ((), (), s32[]{:S(2)}) async-start(), calls=%async_computation.5 | async-start | bytes 31457280 | tf_op jit(solution)/shard_map/all_gather | solution.py:23
  690.1 899.0 %all-reduce.2.cloned.1.call-start = ((), (), s32[]{:S(2)}) async-start(), calls=%async_computation.6 | async-start | bytes 37748736 | tf_op jit(solution)/shard_map/psum | solution.py:27
  1589.1 24.0 %copy-start = (f32[1536,3072]{1,0:T(8,128)S(1)}, f32[1536,3072]{1,0:T(8,128)}, u32[]{:S(2)}) copy-start(f32[1536,3072]{1,0:T(8,128)} %all-reduce.2.cloned.1.call-done) | copy-start | bytes 56623108
Sparse Core Ops, SparseCore 0:
  37.7 416.9 reduce-scatter.1
  540.7 213.8 all-gather.2
  756.2 155.2 all-gather.4
  959.7 629.3 all-reduce.1
where the time goes:
time: 1630 us
  waiting for transfers between devices  1260 us (77%)
  blocking collectives  218 us (13%)
  local copies, waits for them, and re-layouts  68.9 us (4%)
  matrix products  48 us (3%)
  other arithmetic  20.7 us (1%)
    psum x1, waiting for transfers between devices, shards(): gram_tile = lax.psum(partial_tile, 'rep')  630 us
    reduce_scatter x1, waiting for transfers between devices, shards(): lax.psum_scatter(own_part.astype(jnp.bfloat16), 'rep', scatter_dimension=...  417 us
    all_gather x1, waiting for transfers between devices, shards(): lax.all_gather(cols_panel, 'row', axis=0, tiled=True)  146 us
    all_to_all x1, blocking collectives, shards(): lax.all_to_all(summed, 'col', split_axis=1, concat_axis=0, tiled=True)  141 us
    all_to_all x1, blocking collectives, shards(): lax.all_to_all(summed, 'row', split_axis=1, concat_axis=0, tiled=True)  77.3 us
    all_gather x1, waiting for transfers between devices, shards(): left_whole = lax.all_gather(rows_panel, 'col', axis=0, tiled=True)  64.5 us
    dot_general x1, matrix products, shards(): lax.dot_general(left_order, lax.all_gather(cols_panel, 'row', axis=0, til...  48 us
    unnamed x4, local copies, waits for them, and re-layouts  40.5 us
  transfers between devices with their start and end apart: 4, of which 4 were waited for; matrix products, arithmetic and copies ran while one was open for 1% of the time, Pallas kernels for 0%

commit v1 on v0

--- a/solution.py
+++ b/solution.py
@@ -24,7 +24,11 @@
         (((0,), (0,)), ((), ())),
         preferred_element_type=jnp.float32,
     )
-    gram_tile = lax.psum(partial_tile, "rep")
+    gram_tile = partial_tile
+    for hop in (1, 2):
+        gram_tile = gram_tile + lax.ppermute(
+            gram_tile, "rep", [(dev, dev ^ hop) for dev in range(4)]
+        )
     return (gram_tile, 0.95 * statistic + 0.05 * gram_tile)
 
 

time: 1630 us -> 2240 us (1.37)
  waiting for transfers between devices: 1260 us -> 1840 us
  other arithmetic: 20.7 us -> 45.8 us
    ppermute x0 -> x2, waiting for transfers between devices: none -> 1220 us  [shards(): lax.ppermute(gram_tile, 'rep', [(dev, dev ^ hop) for dev in range(4)])]
    psum x1 -> x0, waiting for transfers between devices: 630 us -> none  [shards(): gram_tile = lax.psum(partial_tile, 'rep')]
  transfers between devices with their start and end apart: 4 -> 5, of which waited for: 4 -> 5; matrix products, arithmetic and copies ran while one was open for 1% -> 1% of each run, Pallas kernels for 0% -> 0%
where the time goes in v1:
time: 2240 us
  waiting for transfers between devices  1840 us (82%)
  blocking collectives  218 us (10%)
  local copies, waits for them, and re-layouts  65.5 us (3%)
  matrix products  48 us (2%)
  other arithmetic  45.8 us (2%)
    ppermute x2, waiting for transfers between devices, shards(): lax.ppermute(gram_tile, 'rep', [(dev, dev ^ hop) for dev in range(4)])  1220 us
    reduce_scatter x1, waiting for transfers between devices, shards(): lax.psum_scatter(own_part.astype(jnp.bfloat16), 'rep', scatter_dimension=...  417 us
    all_gather x1, waiting for transfers between devices, shards(): lax.all_gather(cols_panel, 'row', axis=0, tiled=True)  146 us
    all_to_all x1, blocking collectives, shards(): lax.all_to_all(summed, 'col', split_axis=1, concat_axis=0, tiled=True)  141 us
    all_to_all x1, blocking collectives, shards(): lax.all_to_all(summed, 'row', split_axis=1, concat_axis=0, tiled=True)  77.3 us
    all_gather x1, waiting for transfers between devices, shards(): left_whole = lax.all_gather(rows_panel, 'col', axis=0, tiled=True)  64.6 us
    dot_general x1, matrix products, shards(): lax.dot_general(left_order, lax.all_gather(cols_panel, 'row', axis=0, til...  48 us
  transfers between devices with their start and end apart: 5, of which 5 were waited for; matrix products, arithmetic and copies ran while one was open for 1% of the time, Pallas kernels for 0%

profile of v1, /device:TPU:0, one launch (start us, length us, event | category | flops | bytes accessed | tf_op | source)
XLA Modules:
  0.0 2238.2 jit_solution(3496893413869900209)
XLA Ops:
  7.2 0.0 reduce-scatter.2.cloned.1.call-start
  7.2 30.2 %copy.5 = bf16[1,2048,6144]{1,2,0:T(8,128)(2,1)} copy(bf16[1,2048,6144]{2,1,0:T(8,128)(2,1)} %param.2) | data formatting | bytes 50331648 | tf_op args[0]
  37.4 0.0 reduce-scatter.2.cloned.1.call-update
  37.5 0.0 all-gather.3.cloned.1.call-start
  37.5 417.0 %reduce-scatter.2.cloned.1.call-done = bf16[512,6144]{0,1:T(8,128)(2,1)} async-done(((bf16[2048,6144]{0,1:T(8,128)(2,1)}), bf16[512,6144]{0,1:T(8,128)(2,1)}) %reduce-scatter.2.cloned.1.call-update) | async-done | bytes 6291472 | tf_op jit(solution)/shard_map/reduce_scatter | solution.py:9
  454.6 77.3 %all_to_all.38 = bf16[512,4,1536]{0,2,1:T(8,128)(2,1)} all-to-all(bf16[512,4,1536]{0,2,1:T(8,128)(2,1)} %bitcast.14), channel_id=1, replica_groups=mesh['rep'=4,'row'=4,'col'=2] {'row'}, dimensions={1} | all-to-all | bytes 12582912 | tf_op jit(solution)/shard_map/all_to_all | solution.py:10
  531.9 8.6 copy.6
  540.5 0.0 all-gather.3.cloned.1.call-update
  540.5 0.0 all-gather.5.cloned.1.call-start
  540.6 140.7 %all_to_all.39 = bf16[512,2,3072]{0,2,1:T(8,128)(2,1)} all-to-all(bf16[512,2,3072]{0,2,1:T(8,128)(2,1)} %bitcast.15), channel_id=1, replica_groups=mesh['rep'=4,'row'=4,'col'=2] {'col'}, dimensions={1} | all-to-all | bytes 12582912 | tf_op jit(solution)/shard_map/all_to_all | solution.py:11
  681.3 8.7 copy.8
  690.0 0.0 all-gather.5.cloned.1.call-update
  690.0 64.6 %all-gather.3.cloned.1.call-done = bf16[4096,1536]{1,0:T(8,128)(2,1)} async-done(((bf16[2048,1536]{1,0:T(8,128)(2,1)}), bf16[4096,1536]{1,0:T(8,128)(2,1)}) %all-gather.3.cloned.1.call-update) | async-done | bytes 12582928 | tf_op jit(solution)/shard_map/all_gather | solution.py:15
  754.5 11.1 copy.7
  765.7 145.7 %all-gather.5.cloned.1.call-done = bf16[4096,3072]{1,0:T(8,128)(2,1)} async-done(((bf16[1024,3072]{1,0:T(8,128)(2,1)}), bf16[4096,3072]{1,0:T(8,128)(2,1)}) %all-gather.5.cloned.1.call-update) | async-done | bytes 25165840 | tf_op jit(solution)/shard_map/all_gather | solution.py:23
  911.4 48.0 %fusion = f32[1536,3072]{1,0:T(8,128)} fusion(bf16[4096,1536]{1,0:T(8,128)(2,1)} %bitcast.21, bf16[4096,3072]{1,0:T(8,128)(2,1)} %all-gather.5.cloned.1.call-done), kind=kOutput, calls=%fused_computation.1 | convolution fusion | flops 38654705664 | bytes 56623104 | tf_op jit(solution)/shard_map/dot_general | solution.py:21
  959.4 1.5 collective-permute-start
  960.9 406.1 %collective-permute-done = f32[1536,3072]{1,0:T(8,128)} collective-permute-done((f32[1536,3072]{1,0:T(8,128)}, f32[1536,3072]{1,0:T(8,128)}, u32[]{:S(2)}, u32[]{:S(2)}) %collective-permute-start) | collective-permute-done | bytes 18874400 | tf_op jit(solution)/shard_map/ppermute | solution.py:29
  1367.1 12.6 add.11
  1379.7 0.0 copy-start
  1379.7 6.8 copy-done
  1386.5 2.4 collective-permute-start.1
  1388.9 809.5 %collective-permute-done.1 = f32[1536,3072]{1,0:T(8,128)} collective-permute-done((f32[1536,3072]{1,0:T(8,128)S(1)}, f32[1536,3072]{1,0:T(8,128)}, u32[]{:S(2)}, u32[]{:S(2)}) %collective-permute-start.1) | collective-permute-done | bytes 18874400 | tf_op jit(solution)/shard_map/ppermute | solution.py:29
  2198.4 33.2 %multiply_add_fusion = (f32[1536,3072]{1,0:T(8,128)}, f32[1536,3072]{1,0:T(8,128)}) fusion(f32[1536,3072]{1,0:T(8,128)} %param.3, f32[1536,3072]{1,0:T(8,128)} %copy-done, f32[1536,3072]{1,0:T(8,128)} %collective-permute-done.1), kind=kLoop, calls=%fused_computation | loop fusion | flops 18874368 | bytes 94371840 | tf_op jit(solution)/shard_map/add | solution.py:32
Async XLA Ops:
  7.2 447.4 %reduce-scatter.2.cloned.1.call-start = ((), (), s32[]{:S(2)}) async-start(), calls=%async_computation.3 | async-start | bytes 31457280 | tf_op jit(solution)/shard_map/reduce_scatter | solution.py:9
  37.5 717.1 %all-gather.3.cloned.1.call-start = ((), (), s32[]{:S(2)}) async-start(), calls=%async_computation.4 | async-start | bytes 18874368 | tf_op jit(solution)/shard_map/all_gather | solution.py:15
  540.5 370.9 %all-gather.5.cloned.1.call-start = ((), (), s32[]{:S(2)}) async-start(), calls=%async_computation.5 | async-start | bytes 31457280 | tf_op jit(solution)/shard_map/all_gather | solution.py:23
  959.4 407.6 %collective-permute-start = (f32[1536,3072]{1,0:T(8,128)}, f32[1536,3072]{1,0:T(8,128)}, u32[]{:S(2)}, u32[]{:S(2)}) collective-permute-start(f32[1536,3072]{1,0:T(8,128)} %fusion), channel_id=1, source_target_pairs={{0,8},{8,0},{16,24},{24,16},{1,9},{9,1},{17,25},{25,17},{2,10},{10... | collective-permute-start | bytes 56623112 | tf_op jit(solution)/shard_map/ppermute | solution.py:29
  1379.7 6.9 copy-start
  1386.5 811.9 %collective-permute-start.1 = (f32[1536,3072]{1,0:T(8,128)S(1)}, f32[1536,3072]{1,0:T(8,128)}, u32[]{:S(2)}, u32[]{:S(2)}) collective-permute-start(f32[1536,3072]{1,0:T(8,128)S(1)} %add.11), channel_id=1, source_target_pairs={{0,16},{8,24},{16,0},{24,8},{1,17},{9,25},{17,1},{25,9},{2,18},{10... | collective-permute-start | bytes 56623112 | tf_op jit(solution)/shard_map/ppermute | solution.py:29
Sparse Core Ops, SparseCore 0:
  37.6 416.9 reduce-scatter.1
  540.6 213.8 all-gather.2
  756.1 155.2 all-gather.4
